TPU v7x, 256 devices: a whole 4x4x8 slice. The times are simulated.
256 devices in a mesh: seq: 16 (over z_lo, x), head: 16 (over y, z_hi, core).
Axes of the slice: x: 4, y: 4, z: 8 (z_hi: 2, z_lo: 4; z = z_hi * 4 + z_lo), core: 2. Of those that a mesh axis runs over, the one named last changes fastest.
Arguments:
- video_q: bfloat16 [8192, 4096], P(('seq', 'head')), may hold values from -200 to 200
- video_k: bfloat16 [8192, 4096], P(('seq', 'head')), may hold values from -6 to 6
- video_v: bfloat16 [8192, 4096], P(('seq', 'head')), may hold values from -6 to 6
- text_k: bfloat16 [512, 4096], P(None, 'head'), may hold values from -6 to 6
- text_v: bfloat16 [512, 4096], P(None, 'head'), may hold values from -6 to 6
- out_weight: bfloat16 [4096, 5120], P('head'), may hold values from -0.09375 to 0.09375
Outputs:
- video_out: bfloat16 [8192, 5120], P(('seq', 'head'))
All inputs are finite; a program needn't handle non-finite values.
Results may differ from a plain program's by a relative error of at most 0.018.
Values may be sent and summed in bfloat16 or wider, within the bound.
A program may use at most 128 MiB of HBM per device.

v0:
```python
import jax
import jax.numpy as jnp
from jax import lax
from jax.sharding import PartitionSpec as P

HD = 128


def sent_together(arrays, axis, dim, along):
    ends, at = ([], 0)
    for a in arrays[:-1]:
        at += a.shape[along]
        ends.append(at)
    both = jnp.concatenate(arrays, axis=along)
    return tuple(jnp.split(lax.all_gather(both, axis, axis=dim, tiled=True), ends, axis=along))


def as_heads(array):
    return array.reshape(array.shape[0], array.shape[1] // HD, HD)


def scores_of(query_heads, key_heads):
    return jnp.einsum(
        "qhd,khd->hqk", query_heads, key_heads, preferred_element_type=jnp.float32
    ) * HD ** (-0.5)


def weigh_values(scores, row_max, value_heads):
    weights = jnp.exp(scores - row_max[..., None]).astype(jnp.bfloat16)
    totals = jnp.sum(weights.astype(jnp.float32), axis=2)
    summed = jnp.einsum("hqk,khd->hqd", weights, value_heads, preferred_element_type=jnp.float32)
    return (totals, summed)


def local_partial(query_heads, key_heads, value_heads):
    scores = scores_of(query_heads, key_heads)
    row_max = jnp.max(scores, axis=2)
    totals, summed = weigh_values(scores, row_max, value_heads)
    return (row_max, totals, summed)


def combine_partial(first, second):
    joint = jnp.maximum(first[0], second[0])
    first_factor = jnp.exp(first[0] - joint)
    second_factor = jnp.exp(second[0] - joint)
    totals = first[1] * first_factor + second[1] * second_factor
    summed = first[2] * first_factor[..., None] + second[2] * second_factor[..., None]
    return (joint, totals, summed)


def body(video_q, video_k, video_v, text_k, text_v, out_weight):
    queries, key_rows, value_rows = (
        lax.all_to_all(video_q, "head", split_axis=1, concat_axis=0, tiled=True),
        lax.all_to_all(video_k, "head", split_axis=1, concat_axis=0, tiled=True),
        lax.all_to_all(video_v, "head", split_axis=1, concat_axis=0, tiled=True),
    )
    rows_here = queries.shape[0]
    query_heads = as_heads(queries)
    text_part = local_partial(query_heads, as_heads(text_k), as_heads(text_v))
    slab_pair = sent_together((key_rows, value_rows), "seq", 0, 1)
    merged = combine_partial(
        text_part, local_partial(query_heads, as_heads(slab_pair[0]), as_heads(slab_pair[1]))
    )
    normalized = merged[2] / merged[1][..., None]
    attended = normalized.transpose(1, 0, 2).reshape(rows_here, -1).astype(jnp.bfloat16)
    return lax.psum_scatter(
        jnp.dot(attended, out_weight, preferred_element_type=jnp.float32).astype(jnp.bfloat16),
        "head",
        scatter_dimension=0,
        tiled=True,
    )


def solution(mesh):
    in_specs = (
        P(("seq", "head"), None),
        P(("seq", "head"), None),
        P(("seq", "head"), None),
        P(None, "head"),
        P(None, "head"),
        P("head", None),
    )
    out_specs = P(("seq", "head"), None)
    return jax.shard_map(body, mesh=mesh, in_specs=in_specs, out_specs=out_specs, check_vma=False)
```

profile of v0, /device:TPU:2, one launch (start us, length us, event | category | flops | bytes accessed | tf_op | source)
XLA Modules:
  0.0 337.0 jit_solution(15040952302737471222)
XLA Ops:
  6.5 0.0 copy-start
  6.5 0.0 copy-start.3
  6.5 1.8 copy.72
  8.4 11.2 %all-to-all-start.2 = ((bf16[32,16,256]{2,0,1:T(8,128)(2,1)}), bf16[32,16,256]{2,0,1:T(8,128)(2,1)S(1)}, u32[]{:S(2)}, u32[]{:S(2)}) async-start(bf16[32,16,256]{2,0,1:T(8,128)(2,1)} %bitcast.80), calls=%async_computation.2 | async-start | bytes 524288 | tf_op jit(solution)/shard_map/all_to_all | solution.py:55
  19.6 0.0 all-gather.2.cloned.1.call-start
  19.6 1.0 copy.73
  20.6 11.0 %all-to-all-done.2 = bf16[32,16,256]{2,0,1:T(8,128)(2,1)S(1)} async-done(((bf16[32,16,256]{2,0,1:T(8,128)(2,1)}), bf16[32,16,256]{2,0,1:T(8,128)(2,1)S(1)}, u32[]{:S(2)}, u32[]{:S(2)}) %all-to-all-start.2) | async-done | bytes 262176 | tf_op jit(solution)/shard_map/all_to_all | solution.py:55
  31.6 14.6 %all_to_all.54 = bf16[32,16,256]{2,0,1:T(8,128)(2,1)S(1)} all-to-all(bf16[32,16,256]{2,0,1:T(8,128)(2,1)S(1)} %bitcast.86), channel_id=1, replica_groups=mesh['seq'=16,'head'=16] {'head'}, dimensions={1} | all-to-all | bytes 524288 | tf_op jit(solution)/shard_map/all_to_all | solution.py:54
  46.2 0.9 pad_maximum_fusion
  47.1 0.0 all-gather.2.cloned.1.call-update
  47.1 1.7 copy.74
  48.8 3.5 %all-to-all-start = ((bf16[32,16,256]{2,0,1:T(8,128)(2,1)}), bf16[32,16,256]{2,0,1:T(8,128)(2,1)S(1)}, u32[]{:S(2)}, u32[]{:S(2)}) async-start(bf16[32,16,256]{2,0,1:T(8,128)(2,1)} %bitcast.82), calls=%async_computation | async-start | bytes 524288 | tf_op jit(solution)/shard_map/all_to_all | solution.py:53
  52.4 0.0 reduce-scatter.2.cloned.1.call-start
  52.4 1.8 copy.50
  54.2 10.1 %all-to-all-done = bf16[32,16,256]{2,0,1:T(8,128)(2,1)S(1)} async-done(((bf16[32,16,256]{2,0,1:T(8,128)(2,1)}), bf16[32,16,256]{2,0,1:T(8,128)(2,1)S(1)}, u32[]{:S(2)}, u32[]{:S(2)}) %all-to-all-start) | async-done | bytes 262176 | tf_op jit(solution)/shard_map/all_to_all | solution.py:53
  64.3 0.1 reshape.53
  64.4 0.0 copy-done.3
  64.4 0.5 multiply_reduce_fusion
  64.8 0.0 copy-start.1
  64.8 1.3 copy-done.1
  66.2 0.4 convert_reduce_fusion.1
  66.5 82.3 %all-gather.2.cloned.1.call-done = bf16[8192,512]{1,0:T(8,128)(2,1)} async-done(((bf16[512,512]{1,0:T(8,128)(2,1)}), bf16[8192,512]{1,0:T(8,128)(2,1)}) %all-gather.2.cloned.1.call-update) | async-done | bytes 8388624 | tf_op jit(solution)/shard_map/all_gather | solution.py:15
  148.8 5.7 %fusion.27 = (bf16[8192,256]{1,0:T(8,128)(2,1)}, bf16[8192,256]{1,0:T(8,128)(2,1)}) fusion(bf16[8192,512]{1,0:T(8,128)(2,1)} %all-gather.2.cloned.1.call-done), kind=kLoop, calls=%fused_computation.36 | loop fusion | bytes 16777216 | tf_op jit(solution)/shard_map/split | solution.py:15
  154.5 6.4 %copy.45 = bf16[8192,256]{0,1:T(8,128)(2,1)} copy(bf16[8192,256]{1,0:T(8,128)(2,1)} %get-tuple-element.9) | data formatting | bytes 8388608 | tf_op jit(solution)/shard_map/split | solution.py:15
  160.9 6.4 %copy.42 = bf16[8192,256]{0,1:T(8,128)(2,1)} copy(bf16[8192,256]{1,0:T(8,128)(2,1)} %get-tuple-element.8) | data formatting | bytes 8388608 | tf_op jit(solution)/shard_map/split | solution.py:15
  167.3 15.5 %bitcast_reduce_fusion = (f32[2,512]{1,0:T(2,128)S(1)}, f32[2,8192,512]{2,1,0:T(8,128)}) fusion(bf16[8192,2,128]{0,2,1:T(8,128)(2,1)} %bitcast.84, bf16[512,2,128]{2,1,0:T(2,128)(2,1)S(1)} %reshape.53), kind=kOutput, calls=%fused_computation.1 | convolution fusion | flops 2164259840 | bytes 38014976 | tf_op jit(solution)/shard_map/qhd,khd->hqk/dot_general | solution.py:23
  182.8 15.1 %convert_reduce_fusion = f32[2,512]{1,0:T(2,128)S(1)} fusion(f32[2,512]{1,0:T(2,128)S(1)} %get-tuple-element.10, f32[2,8192,512]{2,1,0:T(8,128)} %get-tuple-element.11), kind=kLoop, calls=%fused_computation.4 | loop fusion | flops 41942016 | bytes 33562624 | tf_op jit(solution)/shard_map/reduce_sum | solution.py:30
  197.9 0.0 copy-start.2
  197.9 0.0 copy-start.4
  197.9 15.7 %fusion.11 = f32[512,2,128]{0,2,1:T(8,128)} fusion(bf16[8192,2,128]{0,2,1:T(8,128)(2,1)} %bitcast.83, f32[2,8192,512]{2,1,0:T(8,128)} %get-tuple-element.11, f32[2,512]{1,0:T(2,128)S(1)} %get-tuple-element.10, f32[512,2]{0,1:T(2,128)S(1)} %get-tuple-element.7), kind=kOutput, calls=%fused_computation.16 | convolution fusion | flops 2172780544 | bytes 38281216 | tf_op jit(solution)/shard_map/hqk,khd->hqd/dot_general | solution.py:31
  213.6 0.0 copy-done.2
  213.6 0.0 copy-done.4
  213.6 1.6 fusion.10
  215.2 0.0 copy-done
  215.2 3.9 %convolution_convert_fusion = bf16[512,5120]{1,0:T(8,128)(2,1)} fusion(bf16[512,256]{0,1:T(8,128)(2,1)S(1)} %bitcast.89, bf16[256,5120]{1,0:T(8,128)(2,1)S(1)} %copy-done), kind=kOutput, calls=%fused_computation.5 | convolution fusion | flops 1344798720 | bytes 8126464 | tf_op jit(solution)/shard_map/dot_general | solution.py:67
  219.1 0.0 reduce-scatter.2.cloned.1.call-update
  219.1 111.1 %reduce-scatter.2.cloned.1.call-done = bf16[32,5120]{1,0:T(8,128)(2,1)} async-done(((bf16[512,5120]{1,0:T(8,128)(2,1)}), bf16[32,5120]{1,0:T(8,128)(2,1)}) %reduce-scatter.2.cloned.1.call-update) | async-done | bytes 327696 | tf_op jit(solution)/shard_map/reduce_scatter | solution.py:66
  (1 shorter events, 0.0 us)
Async XLA Ops:
  6.5 208.7 %copy-start = (bf16[256,5120]{1,0:T(8,128)(2,1)S(1)}, bf16[256,5120]{1,0:T(8,128)(2,1)}, u32[]{:S(2)}) copy-start(bf16[256,5120]{1,0:T(8,128)(2,1)} %param.11) | copy-start | bytes 7864324
  6.5 57.8 %copy-start.3 = (bf16[512,256]{1,0:T(8,128)(2,1)S(1)}, bf16[512,256]{1,0:T(8,128)(2,1)}, u32[]{:S(2)}) copy-start(bf16[512,256]{1,0:T(8,128)(2,1)} %param.9) | copy-start | bytes 786436
  8.4 23.2 %all-to-all-start.2 = ((bf16[32,16,256]{2,0,1:T(8,128)(2,1)}), bf16[32,16,256]{2,0,1:T(8,128)(2,1)S(1)}, u32[]{:S(2)}, u32[]{:S(2)}) async-start(bf16[32,16,256]{2,0,1:T(8,128)(2,1)} %bitcast.80), calls=%async_computation.2 | async-start | bytes 524288 | tf_op jit(solution)/shard_map/all_to_all | solution.py:55
  19.6 129.2 %all-gather.2.cloned.1.call-start = ((), (), s32[]{:S(2)}) async-start(), calls=%async_computation.4 | async-start | bytes 8912896 | tf_op jit(solution)/shard_map/all_gather | solution.py:15
  48.8 15.5 %all-to-all-start = ((bf16[32,16,256]{2,0,1:T(8,128)(2,1)}), bf16[32,16,256]{2,0,1:T(8,128)(2,1)S(1)}, u32[]{:S(2)}, u32[]{:S(2)}) async-start(bf16[32,16,256]{2,0,1:T(8,128)(2,1)} %bitcast.82), calls=%async_computation | async-start | bytes 524288 | tf_op jit(solution)/shard_map/all_to_all | solution.py:53
  52.4 277.8 %reduce-scatter.2.cloned.1.call-start = ((), (), s32[]{:S(2)}) async-start(), calls=%async_computation.5 | async-start | bytes 5570560 | tf_op jit(solution)/shard_map/reduce_scatter | solution.py:66
  64.8 1.3 copy-start.1
  197.9 15.7 %copy-start.2 = (f32[2,512,512]{1,2,0:T(8,128)S(1)}, f32[2,512,512]{1,2,0:T(8,128)}, u32[]{:S(2)}) copy-start(f32[2,512,512]{1,2,0:T(8,128)} %copy-done.1) | copy-start | bytes 6291460
  197.9 15.7 %copy-start.4 = (bf16[512,256]{0,1:T(8,128)(2,1)S(1)}, bf16[512,256]{0,1:T(8,128)(2,1)}, u32[]{:S(2)}) copy-start(bf16[512,256]{0,1:T(8,128)(2,1)} %copy.50) | copy-start | bytes 786436
Sparse Core Ops, SparseCore 0:
  47.3 101.4 all-gather.1
  219.2 110.9 reduce-scatter.1
where the time goes:
time: 338 us; the launch traced here: 337 us
  waiting for transfers between devices  214 us (63%)
  matrix products  37.1 us (11%)
  local copies, waits for them, and re-layouts  26.2 us (8%)
  other arithmetic  16.3 us (5%)
  starting transfers between devices  14.8 us (4%)
  blocking collectives  14.6 us (4%)
  between operations  13.5 us (4%)
    reduce_scatter x1, waiting for transfers between devices, body(): lax.psum_scatter(jnp.dot(attended, out_weight, preferred_element_type=jnp...  111 us
    all_gather x1, waiting for transfers between devices, sent_together(): lax.all_gather(both, axis, axis=dim, tiled=True)  82.3 us
    split x3, local copies, waits for them, and re-layouts, sent_together(): jnp.split(lax.all_gather(both, axis, axis=dim, tiled=True), ends, axis=al...  18.5 us
    dot_general x2, matrix products, weigh_values(): jnp.einsum('hqk,khd->hqd', weights, value_heads, preferred_element_type=j...  17.3 us
    dot_general x2, matrix products, scores_of(): jnp.einsum('qhd,khd->hqk', query_heads, key_heads, preferred_element_type...  15.9 us
    reduce_sum x2, other arithmetic, weigh_values(): totals = jnp.sum(weights.astype(jnp.float32), axis=2)  15.4 us
    all_to_all x1, blocking collectives, body(): lax.all_to_all(video_k, 'head', split_axis=1, concat_axis=0, tiled=True)  14.6 us
    all_to_all x1, starting transfers between devices, body(): lax.all_to_all(video_v, 'head', split_axis=1, concat_axis=0, tiled=True)  11.2 us
  transfers between devices with their start and end apart: 4, of which 4 were waited for; matrix products, arithmetic and copies ran while one was open for 2% of the time, Pallas kernels for 0%

commit v1 on v0

v1 whole, which is shorter than its diff:
```python
import functools
import math

import jax
import jax.numpy as jnp
from jax import lax
from jax.experimental import pallas as pl
from jax.experimental.pallas import tpu as pltpu
from jax.sharding import PartitionSpec as P

HD = 128
C2 = HD ** (-0.5) * math.log2(math.e)
BF = jnp.bfloat16
F32 = jnp.float32
MESH = pl.DeviceIdType.MESH
COLS = 1280
CW = 256
NCH = COLS // CW


def kernel(
    q_hbm, k_hbm, v_hbm, tk_hbm, tv_hbm, w_hbm, out_ref,
    qs, ks, vs, qbuf, kbuf, vbuf, tbuf, wbuf, abuf, att, acc, m_ref, l_ref,
    psend, pown, zbuf, osend,
    s_loc, p1_send, p1_recv, x_send, x_recv, d_send, d_recv, t_send, t_recv,
    w_send, w_recv, wd_send, wd_recv, a_send, a_recv, b_send, b_recv,
    z_send, z_recv, o_send, o_recv,
):
    s, h = lax.axis_index("seq"), lax.axis_index("head")
    x, zl = s % 4, s // 4
    y, zh, c = h // 4, (h // 2) % 2, h % 2
    z = zh * 4 + zl
    p = y * 8 + z

    def dev(x1, y1, zh1, zl1, c1):
        return (zl1 * 4 + x1, y1 * 4 + zh1 * 2 + c1)

    left, right = (x + 3) % 4, (x + 1) % 4

    stage = []
    for i, (src, dst) in enumerate(((k_hbm, ks), (v_hbm, vs), (q_hbm, qs))):
        cp = pltpu.make_async_copy(src, dst, s_loc.at[i])
        cp.start()
        stage.append(cp)

    barrier = pltpu.get_barrier_semaphore()

    def greet(i, carry):
        pp = (p + i) % 32
        pl.semaphore_signal(
            barrier, inc=1, device_id=dev(x, pp // 8, (pp // 4) % 2, pp % 4, c), device_id_type=MESH
        )
        return carry

    lax.fori_loop(1, 32, greet, 0)
    for d in (dev(left, y, zh, zl, c), dev(right, y, zh, zl, c), dev(x, y, zh, zl, 1 - c)):
        pl.semaphore_signal(barrier, inc=1, device_id=d, device_id_type=MESH)
    pl.semaphore_wait(barrier, 34)

    def remote(src, dst, ss, rs, device):
        return pltpu.make_async_remote_copy(
            src_ref=src, dst_ref=dst, send_sem=ss, recv_sem=rs, device_id=device, device_id_type=MESH
        )

    partner = dev(x, y, zh, zl, 1 - c)
    krow = pl.multiple_of(p * 32, 32)
    qrow = pl.multiple_of(zl * 256 + (zh * 4 + y) * 32, 32)
    dests = (
        kbuf.at[0, c, pl.ds(krow, 32)],
        vbuf.at[0, c, pl.ds(krow, 32)],
        qbuf.at[pl.ds(qrow, 32)],
    )
    own = []
    for i, src in enumerate((ks, vs, qs)):
        stage[i].wait()

        def send(j, carry, i=i, src=src):
            pp = (p + j) % 32
            col = pl.multiple_of(pp * 128, 128)
            remote(
                src.at[:, pl.ds(col, 128)], dests[i], p1_send.at[i], p1_recv.at[i],
                dev(x, pp // 8, (pp // 4) % 2, pp % 4, c),
            ).start()
            return carry

        lax.fori_loop(1, 32, send, 0)
        cp = pltpu.make_async_copy(
            src.at[:, pl.ds(pl.multiple_of(p * 128, 128), 128)], dests[i], s_loc.at[3 + i]
        )
        cp.start()
        own.append(cp)

    tcol = pl.multiple_of((zl % 2) * 128, 128)
    texts = []
    for i, src in enumerate((tk_hbm, tv_hbm)):
        piece = src.at[:, pl.ds(tcol, 128)]
        cp = remote(piece, tbuf.at[i, c], t_send.at[i], t_recv.at[i], partner)
        cp.start()
        mine = pltpu.make_async_copy(piece, tbuf.at[i, c], s_loc.at[6 + i])
        mine.start()
        texts.append((cp, mine))

    wrow = pl.ds(pl.multiple_of(c * 256, 256), 256)

    def wcols(y1):
        return w_hbm.at[:, pl.ds(pl.multiple_of(y1 * COLS, 128), COLS)]

    wown = pltpu.make_async_copy(wcols(y), wbuf.at[y, wrow], s_loc.at[8])
    wown.start()
    wd = [remote(wcols(y), wbuf.at[y, wrow], wd_send.at[0], wd_recv.at[0], partner)]
    wd[0].start()

    def share(buf, slot):
        return buf.at[slot, c]

    def total_wait(buf, sem):
        pltpu.make_async_copy(buf, buf, sem).wait()

    bufs = (kbuf, vbuf)
    xs = {}
    ds = {}

    def send_x(i, src_slot, dst_slot, to):
        cp = remote(
            share(bufs[i], src_slot), share(bufs[i], dst_slot),
            x_send.at[i, dst_slot], x_recv.at[i, dst_slot], dev(to, y, zh, zl, c),
        )
        cp.start()
        xs[(i, dst_slot)] = cp

    def send_d(i, slot):
        cp = remote(
            share(bufs[i], slot), share(bufs[i], slot), d_send.at[i, slot], d_recv.at[i, slot], partner
        )
        cp.start()
        ds[(i, slot)] = cp

    for i in (0, 1):
        own[i].wait()
        total_wait(bufs[i].at[0, c, pl.ds(0, 31 * 32)], p1_recv.at[i])
        send_x(i, 0, 3, right)
        send_x(i, 0, 1, left)
        send_d(i, 0)

    ws = []
    for dy in range(1, 4):
        y1 = (y + dy) % 4
        cp = remote(wcols(y1), wbuf.at[y, wrow], w_send.at[dy], w_recv.at[dy], dev(x, y1, zh, zl, c))
        cp.start()
        ws.append(cp)

    own[2].wait()
    total_wait(qbuf.at[pl.ds(0, 31 * 32)], p1_recv.at[2])
    for cp, mine in texts:
        mine.wait()
        cp.wait_recv()

    def step(row, keys, values, first):
        rows = pl.ds(row, 256)
        sc = lax.dot_general(
            qbuf[rows, :], keys, (((1,), (1,)), ((), ())), preferred_element_type=F32
        )
        m_cur = jnp.max(sc, axis=1, keepdims=True)
        if first:
            m_new = m_cur
        else:
            m_old = m_ref[rows, :1]
            m_new = jnp.maximum(m_old, m_cur)
        w = jnp.exp2((sc - m_new) * C2)
        tot = jnp.sum(w, axis=1, keepdims=True)
        o = jnp.dot(w.astype(BF), values, preferred_element_type=F32)
        if first:
            acc[rows, :] = o
            l_ref[rows, :] = jnp.broadcast_to(tot, (256, 128))
        else:
            al = jnp.exp2((m_old - m_new) * C2)
            acc[rows, :] = acc[rows, :] * al + o
            l_ref[rows, :] = l_ref[rows, :] * al + tot
        m_ref[rows, :] = jnp.broadcast_to(m_new, (256, 128))

    src_core = zl // 2

    def text_block(qi, carry):
        step(pl.multiple_of(qi * 256, 256), tbuf[0, src_core], tbuf[1, src_core], True)
        return carry

    lax.fori_loop(0, 4, text_block, 0)

    def video_block(row, slot):
        for core in range(2):
            step(row, kbuf[slot, core], vbuf[slot, core], False)

    def all_rows(slot):
        def one(qi, carry):
            video_block(pl.multiple_of(qi * 256, 256), slot)
            return carry

        lax.fori_loop(0, 4, one, 0)

    for i in (0, 1):
        ds[(i, 0)].wait_recv()
    all_rows(0)

    xs[(0, 3)].wait_recv()
    send_x(0, 3, 2, right)
    send_d(0, 3)
    xs[(0, 1)].wait_recv()
    send_d(0, 1)
    xs[(1, 1)].wait_recv()
    send_x(1, 1, 2, left)
    send_d(1, 1)
    xs[(1, 3)].wait_recv()
    send_d(1, 3)
    for i in (0, 1):
        ds[(i, 1)].wait_recv()
    all_rows(1)
    for i in (0, 1):
        ds[(i, 3)].wait_recv()
    all_rows(3)

    wown.wait()
    for dy in range(1, 4):
        ws[dy - 1].wait_recv()
        piece = wbuf.at[(y + 4 - dy) % 4, wrow]
        cp = remote(piece, piece, wd_send.at[dy], wd_recv.at[dy], partner)
        cp.start()
        wd.append(cp)

    for i in (0, 1):
        xs[(i, 2)].wait_recv()
        send_d(i, 2)
    for i in (0, 1):
        ds[(i, 2)].wait_recv()

    bs = []
    asend = []

    def forward(d):
        cols = pl.ds(pl.multiple_of(((zl + 4 - d) % 4) * 128, 128), 128)
        piece = abuf.at[y, :, cols]
        for dy in range(1, 4):
            cp = remote(
                piece, piece, b_send.at[d, dy], b_recv.at[d, dy], dev(x, (y + dy) % 4, zh, zl, c)
            )
            cp.start()
            bs.append(cp)

    mycols = pl.ds(pl.multiple_of(zl * 128, 128), 128)
    for n, d in enumerate((1, 2, 3, 0)):
        zl1 = (zl + d) % 4
        row = pl.multiple_of(zl1 * 256, 256)
        rows = pl.ds(row, 256)
        video_block(row, 2)
        res = (acc[rows, :] / l_ref[rows, :]).astype(BF)
        if d:
            att[rows, :] = res
            cp = remote(
                att.at[rows], abuf.at[y, :, mycols], a_send.at[d], a_recv.at[d], dev(x, y, zh, zl1, c)
            )
            cp.start()
            asend.append(cp)
            if n:
                asend[n - 1].wait_recv()
                forward(n)
        else:
            abuf[y, :, mycols] = res
            asend[2].wait_recv()
            forward(3)
            forward(0)

    for cp in wd:
        cp.wait_recv()
    for cp in bs:
        cp.wait_recv()

    def part(row, n):
        tot = None
        for yy in range(4):
            t = jnp.dot(
                abuf[yy, pl.ds(row, 128), :], wbuf[yy, :, n * CW : (n + 1) * CW],
                preferred_element_type=F32,
            )
            tot = t if tot is None else tot + t
        return tot

    away = pl.multiple_of((1 - zh) * 128, 128)
    home = pl.multiple_of(zh * 128, 128)
    zs = []
    for n in range(NCH):
        psend[n] = part(away, n).astype(BF)
        cp = remote(psend.at[n], zbuf.at[n], z_send.at[n], z_recv.at[n], dev(x, y, 1 - zh, zl, c))
        cp.start()
        zs.append(cp)
    for n in range(NCH):
        pown[n] = part(home, n)
    os = []
    for n in range(NCH):
        zs[n].wait_recv()
        osend[n] = (pown[n] + zbuf[n].astype(F32)).astype(BF)
        for dy in range(1, 4):
            y1 = (y + dy) % 4
            cp = remote(
                osend.at[n, pl.ds(pl.multiple_of(y1 * 32, 32), 32)],
                out_ref.at[:, pl.ds(pl.multiple_of(y * COLS + n * CW, 128), CW)],
                o_send.at[n, dy], o_recv.at[n, dy], dev(x, y1, zh, zl, c),
            )
            cp.start()
            os.append(cp)
        out_ref[:, pl.ds(pl.multiple_of(y * COLS + n * CW, 128), CW)] = osend[
            n, pl.ds(pl.multiple_of(y * 32, 32), 32), :
        ]

    for cp in os:
        cp.wait_recv()
    for i, src in enumerate((kbuf.at[0, c], vbuf.at[0, c], qbuf)):
        total_wait(src.at[pl.ds(0, 31 * 32)], p1_send.at[i])
    for cp in (
        [t[0] for t in texts] + ws + wd + list(xs.values()) + list(ds.values()) + asend + bs + zs + os
    ):
        cp.wait_send()


def body(*args):
    dma = pltpu.SemaphoreType.DMA
    vm = pltpu.VMEM
    return pl.pallas_call(
        kernel,
        out_shape=jax.ShapeDtypeStruct((32, 5120), BF),
        in_specs=[pl.BlockSpec(memory_space=pl.ANY)] * 6,
        out_specs=pl.BlockSpec(memory_space=pltpu.VMEM),
        scratch_shapes=[
            vm((32, 4096), BF), vm((32, 4096), BF), vm((32, 4096), BF),
            vm((1024, 128), BF), vm((4, 2, 1024, 128), BF), vm((4, 2, 1024, 128), BF),
            vm((2, 2, 512, 128), BF), vm((4, 512, COLS), BF), vm((4, 256, 512), BF),
            vm((1024, 128), BF), vm((1024, 128), F32), vm((1024, 128), F32), vm((1024, 128), F32),
            vm((NCH, 128, CW), BF), vm((NCH, 128, CW), F32), vm((NCH, 128, CW), BF), vm((NCH, 128, CW), BF),
            dma((9,)), dma((3,)), dma((3,)), dma((2, 4)), dma((2, 4)), dma((2, 4)), dma((2, 4)),
            dma((2,)), dma((2,)), dma((4,)), dma((4,)), dma((4,)), dma((4,)),
            dma((4,)), dma((4,)), dma((4, 4)), dma((4, 4)),
            dma((NCH,)), dma((NCH,)), dma((NCH, 4)), dma((NCH, 4)),
        ],
        compiler_params=pltpu.CompilerParams(
            collective_id=0, has_side_effects=True, vmem_limit_bytes=60 * 1024 * 1024
        ),
    )(*args)


def solution(mesh):
    rows = P(("seq", "head"), None)
    in_specs = (rows, rows, rows, P(None, "head"), P(None, "head"), P("head", None))
    return jax.shard_map(body, mesh=mesh, in_specs=in_specs, out_specs=rows, check_vma=False)
```

time: 338 us -> 103 us (0.30)
  waiting for transfers between devices: 214 us -> 0 us
  Pallas kernels: 0 us -> 101 us
  matrix products: 37.1 us -> 0 us
  local copies, waits for them, and re-layouts: 26.2 us -> 1.72 us
  other arithmetic: 16.3 us -> 0 us
  starting transfers between devices: 14.8 us -> 0 us
  blocking collectives: 14.6 us -> 0 us
  between operations: 13.5 us -> 0.01 us
    reduce_scatter x1 -> x0, waiting for transfers between devices: 111 us -> none  [body(): lax.psum_scatter(jnp.dot(attended, out_weight, preferred_element_type=jnp...]
    pallas_call x0 -> x1, Pallas kernels: none -> 101 us  [body(): pl.pallas_call(kernel, out_shape=jax.ShapeDtypeStruct((32, 5120), BF), in...]
    all_gather x1 -> x0, waiting for transfers between devices: 82.3 us -> none  [sent_together(): lax.all_gather(both, axis, axis=dim, tiled=True)]
    dot_general x5 -> x0, matrix products: 37.1 us -> none  [the longest x2 17.3 us: weigh_values(): jnp.einsum('hqk,khd->hqd', weights, value_heads, preferred_element_type=j...]
    all_to_all x2 -> x0, waiting for transfers between devices: 21.1 us -> none  [the longest x1 11 us: body(): lax.all_to_all(video_v, 'head', split_axis=1, concat_axis=0, tiled=True)]
    split x3 -> x0, local copies, waits for them, and re-layouts: 18.5 us -> none  [sent_together(): jnp.split(lax.all_gather(both, axis, axis=dim, tiled=True), ends, axis=al...]
    reduce_sum x2 -> x0, other arithmetic: 15.4 us -> none  [weigh_values(): totals = jnp.sum(weights.astype(jnp.float32), axis=2)]
    all_to_all x2 -> x0, starting transfers between devices: 14.7 us -> none  [the longest x1 11.2 us: body(): lax.all_to_all(video_v, 'head', split_axis=1, concat_axis=0, tiled=True)]
  transfers between devices with their start and end apart: 4 -> 0, of which waited for: 4 -> 0; matrix products, arithmetic and copies ran while one was open for 2% -> 0% of each run, Pallas kernels for 0% -> 0%
where the time goes in v1:
time: 103 us
  Pallas kernels  101 us (98%)
  local copies, waits for them, and re-layouts  1.72 us (2%)
    pallas_call x1, Pallas kernels, body(): pl.pallas_call(kernel, out_shape=jax.ShapeDtypeStruct((32, 5120), BF), in...  101 us

profile of v1, /device:TPU:2, one launch (start us, length us, event | category | flops | bytes accessed | tf_op | source)
XLA Modules:
  0.0 103.0 jit_solution(14606275910022205983)
XLA Ops:
  0.0 101.2 %shard_map.64 = bf16[32,5120]{1,0:T(8,128)(2,1)} custom-call(bf16[32,4096]{1,0:T(8,128)(2,1)} %q_hbm.1, bf16[32,4096]{1,0:T(8,128)(2,1)} %k_hbm.1, bf16[32,4096]{1,0:T(8,128)(2,1)} %v_hbm.1, bf16[512,256]{1,0:T(8,128)(2,1)} %tk_hbm.1, bf16[512,256]{1,0:T(8,128)(2,1)} %tv_hbm.1, bf16[256,5120]{1,0:T(8,128)(2,1)} %w_hbm.1), custom_call_target="tpu_custom_call" | custom-call | tf_op jit(solution)/shard_map/pallas_call | solution.py:326
  101.2 1.7 %copy.8 = bf16[32,5120]{1,0:T(8,128)(2,1)} copy(bf16[32,5120]{1,0:T(8,128)(2,1)} %shard_map.64) | data formatting | bytes 655360

commit v2 on v1

v2 whole, which is shorter than its diff:
```python
import functools
import math

import jax
import jax.numpy as jnp
from jax import lax
from jax.experimental import pallas as pl
from jax.experimental.pallas import tpu as pltpu
from jax.sharding import PartitionSpec as P

HD = 128
C2 = HD ** (-0.5) * math.log2(math.e)
BF = jnp.bfloat16
F32 = jnp.float32
MESH = pl.DeviceIdType.MESH
COLS = 1280
CW = 256
NCH = COLS // CW


def kernel(
    q_hbm, k_hbm, v_hbm, tk_hbm, tv_hbm, w_hbm, out_ref,
    qs, ks, vs, qbuf, kbuf, vbuf, tbuf, wbuf, abuf, att, acc, m_ref, l_ref,
    psend, pown, zbuf, osend,
    s_loc, p1_send, p1_recv, x_send, x_recv, d_send, d_recv, t_send, t_recv,
    w_send, w_recv, wd_send, wd_recv, a_send, a_recv, b_send, b_recv,
    z_send, z_recv, o_send, o_recv,
):
    s, h = lax.axis_index("seq"), lax.axis_index("head")
    x, zl = s % 4, s // 4
    y, zh, c = h // 4, (h // 2) % 2, h % 2
    z = zh * 4 + zl
    p = y * 8 + z

    def dev(x1, y1, zh1, zl1, c1):
        return (zl1 * 4 + x1, y1 * 4 + zh1 * 2 + c1)

    left, right = (x + 3) % 4, (x + 1) % 4

    stage = []
    for i, (src, dst) in enumerate(((k_hbm, ks), (v_hbm, vs), (q_hbm, qs))):
        cp = pltpu.make_async_copy(src, dst, s_loc.at[i])
        cp.start()
        stage.append(cp)

    barrier = pltpu.get_barrier_semaphore()

    def greet(i, carry):
        pp = (p + i) % 32
        pl.semaphore_signal(
            barrier, inc=1, device_id=dev(x, pp // 8, (pp // 4) % 2, pp % 4, c), device_id_type=MESH
        )
        return carry

    lax.fori_loop(1, 32, greet, 0)
    for d in (dev(left, y, zh, zl, c), dev(right, y, zh, zl, c), dev(x, y, zh, zl, 1 - c)):
        pl.semaphore_signal(barrier, inc=1, device_id=d, device_id_type=MESH)
    pl.semaphore_wait(barrier, 34)

    def remote(src, dst, ss, rs, device):
        return pltpu.make_async_remote_copy(
            src_ref=src, dst_ref=dst, send_sem=ss, recv_sem=rs, device_id=device, device_id_type=MESH
        )

    partner = dev(x, y, zh, zl, 1 - c)
    qrow = pl.multiple_of(zh * 512 + zl * 128 + y * 32, 32)
    stages = {0: ks, 1: vs, 2: qs}
    bufs = (kbuf, vbuf)

    def send_half(i, half):
        def send(j, carry):
            dz, dy = (j // 4) * 2 + half, j % 4
            y1, z1 = (y + dy) % 4, (z + dz) % 8
            col = pl.multiple_of((y1 * 8 + z1) * 128, 128)
            row = pl.multiple_of(half * 512 + j * 32, 32)
            dst = qbuf.at[pl.ds(qrow, 32)] if i == 2 else bufs[i].at[0, c, pl.ds(row, 32)]
            remote(
                stages[i].at[:, pl.ds(col, 128)], dst, p1_send.at[i, half], p1_recv.at[i, half],
                dev(x, y1, z1 // 4, z1 % 4, c),
            ).start()
            return carry

        lax.fori_loop(1 - half, 16, send, 0)

    mycol = pl.ds(pl.multiple_of(p * 128, 128), 128)
    own = {}
    for i, half in ((0, 0), (1, 0), (2, 0), (2, 1), (0, 1), (1, 1)):
        if half == 0:
            stage[i].wait()
        send_half(i, half)
        if half == 0:
            dst = qbuf.at[pl.ds(qrow, 32)] if i == 2 else bufs[i].at[0, c, pl.ds(0, 32)]
            cp = pltpu.make_async_copy(stages[i].at[:, mycol], dst, s_loc.at[3 + i])
            cp.start()
            own[i] = cp

    tcol = pl.multiple_of((zl % 2) * 128, 128)
    texts = []
    for i, src in enumerate((tk_hbm, tv_hbm)):
        piece = src.at[:, pl.ds(tcol, 128)]
        cp = remote(piece, tbuf.at[i, c], t_send.at[i], t_recv.at[i], partner)
        cp.start()
        mine = pltpu.make_async_copy(piece, tbuf.at[i, c], s_loc.at[6 + i])
        mine.start()
        texts.append((cp, mine))

    wrow = pl.ds(pl.multiple_of(c * 256, 256), 256)

    def wcols(y1):
        return w_hbm.at[:, pl.ds(pl.multiple_of(y1 * COLS, 128), COLS)]

    wown = pltpu.make_async_copy(wcols(y), wbuf.at[y, wrow], s_loc.at[8])
    wown.start()
    wd = [remote(wcols(y), wbuf.at[y, wrow], wd_send.at[0], wd_recv.at[0], partner)]
    wd[0].start()
    ws = {}
    for dy in (2, 1, 3):
        y1 = (y + dy) % 4
        ws[dy] = remote(wcols(y1), wbuf.at[y, wrow], w_send.at[dy], w_recv.at[dy], dev(x, y1, zh, zl, c))
        ws[dy].start()

    def total_wait(buf, sem):
        pltpu.make_async_copy(buf, buf, sem).wait()

    xs, ds = {}, {}

    def share(i, half, slot):
        return bufs[i].at[slot, c, pl.ds(half * 512, 512)]

    def send_x(i, half, src_slot, dst_slot, to):
        cp = remote(
            share(i, half, src_slot), share(i, half, dst_slot),
            x_send.at[i, half, dst_slot], x_recv.at[i, half, dst_slot], dev(to, y, zh, zl, c),
        )
        cp.start()
        xs[(i, half, dst_slot)] = cp

    def send_d(i, half, slot):
        cp = remote(
            share(i, half, slot), share(i, half, slot),
            d_send.at[i, half, slot], d_recv.at[i, half, slot], partner,
        )
        cp.start()
        ds[(i, half, slot)] = cp

    def arrive_own(i, half):
        if half == 0:
            own[i].wait()
        n = 480 if half == 0 else 512
        total_wait(bufs[i].at[0, c, pl.ds(0, n)], p1_recv.at[i, half])
        send_x(i, half, 0, 3, right)
        send_x(i, half, 0, 1, left)
        send_d(i, half, 0)

    def arrive_near(i, half):
        first, second = (3, 1) if i == 0 else (1, 3)
        xs[(i, half, first)].wait_recv()
        send_x(i, half, first, 2, right if i == 0 else left)
        send_d(i, half, first)
        xs[(i, half, second)].wait_recv()
        send_d(i, half, second)

    def arrive_far(half):
        for i in (0, 1):
            xs[(i, half, 2)].wait_recv()
            send_d(i, half, 2)

    def arrive_core(half, slot):
        for i in (0, 1):
            ds[(i, half, slot)].wait_recv()

    def step(row, pieces, first):
        rows = pl.ds(row, 256)
        q = qbuf[rows, :]
        scs = [
            lax.dot_general(q, kk(), (((1,), (1,)), ((), ())), preferred_element_type=F32)
            for kk, vv in pieces
        ]
        m_new = functools.reduce(jnp.maximum, [jnp.max(sc, axis=1, keepdims=True) for sc in scs])
        if not first:
            m_old = m_ref[rows, :1]
            m_new = jnp.maximum(m_old, m_new)
        tot, o = 0.0, 0.0
        for sc, (kk, vv) in zip(scs, pieces):
            w = jnp.exp2((sc - m_new) * C2)
            tot = tot + jnp.sum(w, axis=1, keepdims=True)
            o = o + jnp.dot(w.astype(BF), vv(), preferred_element_type=F32)
        if first:
            acc[rows, :] = o
            l_ref[rows, :] = jnp.broadcast_to(tot, (256, 128))
        else:
            al = jnp.exp2((m_old - m_new) * C2)
            acc[rows, :] = acc[rows, :] * al + o
            l_ref[rows, :] = l_ref[rows, :] * al + tot
        m_ref[rows, :] = jnp.broadcast_to(m_new, (256, 128))

    src_core = zl // 2
    text_piece = (lambda: tbuf[0, src_core], lambda: tbuf[1, src_core])

    def video_pieces(half, slot):
        hr = pl.ds(half * 512, 512)
        return [
            (lambda core=core: kbuf[slot, core, hr], lambda core=core: vbuf[slot, core, hr])
            for core in range(2)
        ]

    def all_rows(pieces, first=False):
        def one(qi, carry):
            step(pl.multiple_of(qi * 256, 256), pieces, first)
            return carry

        lax.fori_loop(0, 4, one, 0)

    arrive_own(0, 0)
    arrive_own(1, 0)
    arrive_near(0, 0)
    arrive_near(1, 0)
    own[2].wait()
    total_wait(qbuf.at[pl.ds(0, 480)], p1_recv.at[2, 0])
    total_wait(qbuf.at[pl.ds(0, 512)], p1_recv.at[2, 1])
    for cp, mine in texts:
        mine.wait()
        cp.wait_recv()
    all_rows([text_piece], True)
    arrive_core(0, 0)
    all_rows(video_pieces(0, 0))
    arrive_own(0, 1)
    arrive_far(0)
    arrive_core(0, 1)
    all_rows(video_pieces(0, 1))
    arrive_own(1, 1)
    arrive_core(0, 3)
    all_rows(video_pieces(0, 3))
    arrive_near(0, 1)
    arrive_core(0, 2)
    all_rows(video_pieces(0, 2))
    arrive_near(1, 1)
    arrive_core(1, 0)
    all_rows(video_pieces(1, 0))
    arrive_core(1, 1)
    all_rows(video_pieces(1, 1))
    arrive_far(1)
    arrive_core(1, 3)
    all_rows(video_pieces(1, 3))

    wown.wait()
    for dy in (2, 1, 3):
        ws[dy].wait_recv()
        piece = wbuf.at[(y + 4 - dy) % 4, wrow]
        cp = remote(piece, piece, wd_send.at[dy], wd_recv.at[dy], partner)
        cp.start()
        wd.append(cp)
    arrive_core(1, 2)

    aas, bs = {}, {}
    mycols = pl.ds(pl.multiple_of(zl * 128, 128), 128)

    def last_rows(zhalf, k):
        row = pl.multiple_of(zhalf * 512 + k * 256, 256)
        step(row, video_pieces(1, 2), False)
        rows = pl.ds(row, 256)
        att[rows, :] = (acc[rows, :] / l_ref[rows, :]).astype(BF)

    def send_att(zhalf, k):
        for d in range(1, 4):
            zl1 = (zl + d) % 4
            rows = pl.ds(pl.multiple_of(zhalf * 512 + zl1 * 128, 128), 128)
            cp = remote(
                att.at[rows], abuf.at[zhalf, y, :, mycols], a_send.at[k, d], a_recv.at[k, d],
                dev(x, y, zh, zl1, c),
            )
            cp.start()
            aas[(k, d)] = cp
        rows = pl.ds(pl.multiple_of(zhalf * 512 + zl * 128, 128), 128)
        abuf[zhalf, y, :, mycols] = att[rows, :]

    def send_b(zhalf, k):
        for d in range(1, 4):
            aas[(k, d)].wait_recv()
        piece = abuf.at[zhalf, y]
        for dy in (2, 1, 3):
            cp = remote(
                piece, piece, b_send.at[k, dy], b_recv.at[k, dy], dev(x, (y + dy) % 4, zh, zl, c)
            )
            cp.start()
            bs[(k, dy)] = cp

    away, home = 1 - zh, zh
    last_rows(away, 0)
    last_rows(away, 1)
    send_att(away, 0)
    last_rows(home, 0)
    last_rows(home, 1)
    send_att(home, 1)
    send_b(away, 0)
    send_b(home, 1)

    for cp in wd:
        cp.wait_recv()

    def part(zhalf, n):
        tot = None
        for yy in range(4):
            t = jnp.dot(
                abuf[zhalf, yy], wbuf[yy, :, n * CW : (n + 1) * CW], preferred_element_type=F32
            )
            tot = t if tot is None else tot + t
        return tot

    for dy in range(1, 4):
        bs[(0, dy)].wait_recv()
    zs = []
    for n in range(NCH):
        psend[n] = part(away, n).astype(BF)
        cp = remote(psend.at[n], zbuf.at[n], z_send.at[n], z_recv.at[n], dev(x, y, 1 - zh, zl, c))
        cp.start()
        zs.append(cp)
    for dy in range(1, 4):
        bs[(1, dy)].wait_recv()
    for n in range(NCH):
        pown[n] = part(home, n)
    os = []
    for n in range(NCH):
        zs[n].wait_recv()
        osend[n] = (pown[n] + zbuf[n].astype(F32)).astype(BF)
        for dy in (2, 1, 3):
            y1 = (y + dy) % 4
            cp = remote(
                osend.at[n, pl.ds(pl.multiple_of(y1 * 32, 32), 32)],
                out_ref.at[:, pl.ds(pl.multiple_of(y * COLS + n * CW, 128), CW)],
                o_send.at[n, dy], o_recv.at[n, dy], dev(x, y1, zh, zl, c),
            )
            cp.start()
            os.append(cp)
        out_ref[:, pl.ds(pl.multiple_of(y * COLS + n * CW, 128), CW)] = osend[
            n, pl.ds(pl.multiple_of(y * 32, 32), 32), :
        ]

    for cp in os:
        cp.wait_recv()
    for i in range(3):
        for half in range(2):
            n = 480 if half == 0 else 512
            total_wait(qbuf.at[pl.ds(0, n)], p1_send.at[i, half])
    for cp in (
        [t[0] for t in texts] + list(ws.values()) + wd + list(xs.values()) + list(ds.values())
        + list(aas.values()) + list(bs.values()) + zs + os
    ):
        cp.wait_send()


def body(*args):
    dma = pltpu.SemaphoreType.DMA
    vm = pltpu.VMEM
    return pl.pallas_call(
        kernel,
        out_shape=jax.ShapeDtypeStruct((32, 5120), BF),
        in_specs=[pl.BlockSpec(memory_space=pl.ANY)] * 6,
        out_specs=pl.BlockSpec(memory_space=pltpu.VMEM),
        scratch_shapes=[
            vm((32, 4096), BF), vm((32, 4096), BF), vm((32, 4096), BF),
            vm((1024, 128), BF), vm((4, 2, 1024, 128), BF), vm((4, 2, 1024, 128), BF),
            vm((2, 2, 512, 128), BF), vm((4, 512, COLS), BF), vm((2, 4, 128, 512), BF),
            vm((1024, 128), BF), vm((1024, 128), F32), vm((1024, 128), F32), vm((1024, 128), F32),
            vm((NCH, 128, CW), BF), vm((NCH, 128, CW), F32), vm((NCH, 128, CW), BF), vm((NCH, 128, CW), BF),
            dma((9,)), dma((3, 2)), dma((3, 2)), dma((2, 2, 4)), dma((2, 2, 4)), dma((2, 2, 4)), dma((2, 2, 4)),
            dma((2,)), dma((2,)), dma((4,)), dma((4,)), dma((4,)), dma((4,)),
            dma((2, 4)), dma((2, 4)), dma((2, 4)), dma((2, 4)),
            dma((NCH,)), dma((NCH,)), dma((NCH, 4)), dma((NCH, 4)),
        ],
        compiler_params=pltpu.CompilerParams(
            collective_id=0, has_side_effects=True, vmem_limit_bytes=60 * 1024 * 1024
        ),
    )(*args)


def solution(mesh):
    rows = P(("seq", "head"), None)
    in_specs = (rows, rows, rows, P(None, "head"), P(None, "head"), P("head", None))
    return jax.shard_map(body, mesh=mesh, in_specs=in_specs, out_specs=rows, check_vma=False)
```

time: 103 us -> 86.5 us (0.84)
  the two profiles are of different devices: /device:TPU:2 before, /device:TPU:32 now
where the time goes in v2:
time: 86.5 us; the launch traced here: 86.4 us
  Pallas kernels  84.7 us (98%)
  local copies, waits for them, and re-layouts  1.72 us (2%)
    pallas_call x1, Pallas kernels, body(): pl.pallas_call(kernel, out_shape=jax.ShapeDtypeStruct((32, 5120), BF), in...  84.7 us

profile of v2, /device:TPU:32, one launch (start us, length us, event | category | flops | bytes accessed | tf_op | source)
XLA Modules:
  0.0 86.4 jit_solution(7306570558526985862)
XLA Ops:
  0.0 84.7 %shard_map.64 = bf16[32,5120]{1,0:T(8,128)(2,1)} custom-call(bf16[32,4096]{1,0:T(8,128)(2,1)} %q_hbm.1, bf16[32,4096]{1,0:T(8,128)(2,1)} %k_hbm.1, bf16[32,4096]{1,0:T(8,128)(2,1)} %v_hbm.1, bf16[512,256]{1,0:T(8,128)(2,1)} %tk_hbm.1, bf16[512,256]{1,0:T(8,128)(2,1)} %tv_hbm.1, bf16[256,5120]{1,0:T(8,128)(2,1)} %w_hbm.1), custom_call_target="tpu_custom_call" | custom-call | tf_op jit(solution)/shard_map/pallas_call | solution.py:355
  84.7 1.7 %copy.8 = bf16[32,5120]{1,0:T(8,128)(2,1)} copy(bf16[32,5120]{1,0:T(8,128)(2,1)} %shard_map.64) | data formatting | bytes 655360

commit v3 on v2

--- a/solution.py
+++ b/solution.py
@@ -14,6 +14,7 @@
 F32 = jnp.float32
 MESH = pl.DeviceIdType.MESH
 COLS = 1280
+QB = 512
 CW = 256
 NCH = COLS // CW
 
@@ -114,10 +115,25 @@
     wd = [remote(wcols(y), wbuf.at[y, wrow], wd_send.at[0], wd_recv.at[0], partner)]
     wd[0].start()
     ws = {}
-    for dy in (2, 1, 3):
+    pair = zl + 1 - 2 * (zl % 2)
+    hrow = pl.multiple_of((zl % 2) * 128, 128)
+    y2 = (y + 2) % 4
+    ws[2] = remote(
+        w_hbm.at[pl.ds(hrow, 128), pl.ds(pl.multiple_of(y2 * COLS, 128), COLS)],
+        wbuf.at[y, pl.ds(pl.multiple_of(c * 256 + hrow, 128), 128)],
+        w_send.at[2], w_recv.at[2], dev(x, y2, zh, zl, c),
+    )
+    ws[2].start()
+    for dy in (1, 3):
         y1 = (y + dy) % 4
         ws[dy] = remote(wcols(y1), wbuf.at[y, wrow], w_send.at[dy], w_recv.at[dy], dev(x, y1, zh, zl, c))
         ws[dy].start()
+
+    def pass_pair():
+        ws[2].wait_recv()
+        piece = wbuf.at[y2, pl.ds(pl.multiple_of(c * 256 + hrow, 128), 128)]
+        ws[4] = remote(piece, piece, w_send.at[4], w_recv.at[4], dev(x, y, zh, pair, c))
+        ws[4].start()
 
     def total_wait(buf, sem):
         pltpu.make_async_copy(buf, buf, sem).wait()
@@ -169,30 +185,37 @@
         for i in (0, 1):
             ds[(i, half, slot)].wait_recv()
 
-    def step(row, pieces, first):
-        rows = pl.ds(row, 256)
+    def step(row, nrow, pieces, first):
+        rows = pl.ds(row, nrow)
         q = qbuf[rows, :]
         scs = [
             lax.dot_general(q, kk(), (((1,), (1,)), ((), ())), preferred_element_type=F32)
             for kk, vv in pieces
         ]
-        m_new = functools.reduce(jnp.maximum, [jnp.max(sc, axis=1, keepdims=True) for sc in scs])
-        if not first:
-            m_old = m_ref[rows, :1]
+        lanes = [sc[:, i : i + 128] for sc in scs for i in range(0, sc.shape[1], 128)]
+        m_new = jnp.max(functools.reduce(jnp.maximum, lanes), axis=1, keepdims=True)
+        if first:
+            m_new = jnp.broadcast_to(m_new, (nrow, 128))
+        else:
+            m_old = m_ref[rows, :]
             m_new = jnp.maximum(m_old, m_new)
-        tot, o = 0.0, 0.0
+        tot, o = None, None
         for sc, (kk, vv) in zip(scs, pieces):
-            w = jnp.exp2((sc - m_new) * C2)
-            tot = tot + jnp.sum(w, axis=1, keepdims=True)
-            o = o + jnp.dot(w.astype(BF), vv(), preferred_element_type=F32)
+            ws = []
+            for i in range(0, sc.shape[1], 128):
+                w = jnp.exp2((sc[:, i : i + 128] - m_new) * C2)
+                tot = w if tot is None else tot + w
+                ws.append(w.astype(BF))
+            part_o = jnp.dot(jnp.concatenate(ws, axis=1), vv(), preferred_element_type=F32)
+            o = part_o if o is None else o + part_o
         if first:
             acc[rows, :] = o
-            l_ref[rows, :] = jnp.broadcast_to(tot, (256, 128))
+            l_ref[rows, :] = tot
         else:
             al = jnp.exp2((m_old - m_new) * C2)
             acc[rows, :] = acc[rows, :] * al + o
             l_ref[rows, :] = l_ref[rows, :] * al + tot
-        m_ref[rows, :] = jnp.broadcast_to(m_new, (256, 128))
+        m_ref[rows, :] = m_new
 
     src_core = zl // 2
     text_piece = (lambda: tbuf[0, src_core], lambda: tbuf[1, src_core])
@@ -206,10 +229,10 @@
 
     def all_rows(pieces, first=False):
         def one(qi, carry):
-            step(pl.multiple_of(qi * 256, 256), pieces, first)
+            step(pl.multiple_of(qi * QB, QB), QB, pieces, first)
             return carry
 
-        lax.fori_loop(0, 4, one, 0)
+        lax.fori_loop(0, 1024 // QB, one, 0)
 
     arrive_own(0, 0)
     arrive_own(1, 0)
@@ -229,6 +252,7 @@
     arrive_core(0, 1)
     all_rows(video_pieces(0, 1))
     arrive_own(1, 1)
+    pass_pair()
     arrive_core(0, 3)
     all_rows(video_pieces(0, 3))
     arrive_near(0, 1)
@@ -245,7 +269,7 @@
 
     wown.wait()
     for dy in (2, 1, 3):
-        ws[dy].wait_recv()
+        ws[4 if dy == 2 else dy].wait_recv()
         piece = wbuf.at[(y + 4 - dy) % 4, wrow]
         cp = remote(piece, piece, wd_send.at[dy], wd_recv.at[dy], partner)
         cp.start()
@@ -255,11 +279,11 @@
     aas, bs = {}, {}
     mycols = pl.ds(pl.multiple_of(zl * 128, 128), 128)
 
-    def last_rows(zhalf, k):
-        row = pl.multiple_of(zhalf * 512 + k * 256, 256)
-        step(row, video_pieces(1, 2), False)
-        rows = pl.ds(row, 256)
-        att[rows, :] = (acc[rows, :] / l_ref[rows, :]).astype(BF)
+    def last_rows(zhalf):
+        row = pl.multiple_of(zhalf * 512, 512)
+        step(row, 512, video_pieces(1, 2), False)
+        rows = pl.ds(row, 512)
+        att[rows, :] = (acc[rows, :] / jnp.sum(l_ref[rows, :], axis=1, keepdims=True)).astype(BF)
 
     def send_att(zhalf, k):
         for d in range(1, 4):
@@ -286,11 +310,9 @@
             bs[(k, dy)] = cp
 
     away, home = 1 - zh, zh
-    last_rows(away, 0)
-    last_rows(away, 1)
+    last_rows(away)
     send_att(away, 0)
-    last_rows(home, 0)
-    last_rows(home, 1)
+    last_rows(home)
     send_att(home, 1)
     send_b(away, 0)
     send_b(home, 1)
@@ -364,7 +386,7 @@
             vm((1024, 128), BF), vm((1024, 128), F32), vm((1024, 128), F32), vm((1024, 128), F32),
             vm((NCH, 128, CW), BF), vm((NCH, 128, CW), F32), vm((NCH, 128, CW), BF), vm((NCH, 128, CW), BF),
             dma((9,)), dma((3, 2)), dma((3, 2)), dma((2, 2, 4)), dma((2, 2, 4)), dma((2, 2, 4)), dma((2, 2, 4)),
-            dma((2,)), dma((2,)), dma((4,)), dma((4,)), dma((4,)), dma((4,)),
+            dma((2,)), dma((2,)), dma((5,)), dma((5,)), dma((4,)), dma((4,)),
             dma((2, 4)), dma((2, 4)), dma((2, 4)), dma((2, 4)),
             dma((NCH,)), dma((NCH,)), dma((NCH, 4)), dma((NCH, 4)),
         ],

time: 86.5 us -> 79.7 us (0.921)
  the two profiles are of different devices: /device:TPU:32 before, /device:TPU:2 now
where the time goes in v3:
time: 79.7 us; the launch traced here: 79.6 us
  Pallas kernels  77.9 us (98%)
  local copies, waits for them, and re-layouts  1.72 us (2%)
    pallas_call x1, Pallas kernels, body(): pl.pallas_call(kernel, out_shape=jax.ShapeDtypeStruct((32, 5120), BF), in...  77.9 us
    unnamed x1, local copies, waits for them, and re-layouts  1.72 us

profile of v3, /device:TPU:2, one launch (start us, length us, event | category | flops | bytes accessed | tf_op | source)
XLA Modules:
  0.0 79.6 jit_solution(18145571490276790559)
XLA Ops:
  0.0 77.9 %shard_map.64 = bf16[32,5120]{1,0:T(8,128)(2,1)} custom-call(bf16[32,4096]{1,0:T(8,128)(2,1)} %q_hbm.1, bf16[32,4096]{1,0:T(8,128)(2,1)} %k_hbm.1, bf16[32,4096]{1,0:T(8,128)(2,1)} %v_hbm.1, bf16[512,256]{1,0:T(8,128)(2,1)} %tk_hbm.1, bf16[512,256]{1,0:T(8,128)(2,1)} %tv_hbm.1, bf16[256,5120]{1,0:T(8,128)(2,1)} %w_hbm.1), custom_call_target="tpu_custom_call" | custom-call | tf_op jit(solution)/shard_map/pallas_call | solution.py:377
  77.9 1.7 %copy.8 = bf16[32,5120]{1,0:T(8,128)(2,1)} copy(bf16[32,5120]{1,0:T(8,128)(2,1)} %shard_map.64) | data formatting | bytes 655360

commit v4 on v3

--- a/solution.py
+++ b/solution.py
@@ -227,12 +227,12 @@
             for core in range(2)
         ]
 
-    def all_rows(pieces, first=False):
-        def one(qi, carry):
-            step(pl.multiple_of(qi * QB, QB), QB, pieces, first)
-            return carry
-
-        lax.fori_loop(0, 1024 // QB, one, 0)
+    away, home = 1 - zh, zh
+
+    def attend(zhalf, half, slot):
+        first = half == 0 and slot == 0
+        pieces = ([text_piece] if first else []) + video_pieces(half, slot)
+        step(pl.multiple_of(zhalf * 512, 512), 512, pieces, first)
 
     arrive_own(0, 0)
     arrive_own(1, 0)
@@ -244,31 +244,35 @@
     for cp, mine in texts:
         mine.wait()
         cp.wait_recv()
-    all_rows([text_piece], True)
     arrive_core(0, 0)
-    all_rows(video_pieces(0, 0))
+    attend(away, 0, 0)
+    attend(home, 0, 0)
     arrive_own(0, 1)
     arrive_far(0)
     arrive_core(0, 1)
-    all_rows(video_pieces(0, 1))
+    attend(away, 0, 1)
+    attend(home, 0, 1)
     arrive_own(1, 1)
+    arrive_core(0, 3)
+    attend(away, 0, 3)
+    arrive_near(0, 1)
+    attend(home, 0, 3)
     pass_pair()
-    arrive_core(0, 3)
-    all_rows(video_pieces(0, 3))
-    arrive_near(0, 1)
     arrive_core(0, 2)
-    all_rows(video_pieces(0, 2))
+    attend(away, 0, 2)
+    attend(home, 0, 2)
     arrive_near(1, 1)
     arrive_core(1, 0)
-    all_rows(video_pieces(1, 0))
+    attend(away, 1, 0)
+    attend(home, 1, 0)
     arrive_core(1, 1)
-    all_rows(video_pieces(1, 1))
+    attend(away, 1, 1)
+    arrive_core(1, 3)
+    attend(away, 1, 3)
     arrive_far(1)
-    arrive_core(1, 3)
-    all_rows(video_pieces(1, 3))
-
+    attend(home, 1, 1)
     wown.wait()
-    for dy in (2, 1, 3):
+    for dy in (1, 3, 2):
         ws[4 if dy == 2 else dy].wait_recv()
         piece = wbuf.at[(y + 4 - dy) % 4, wrow]
         cp = remote(piece, piece, wd_send.at[dy], wd_recv.at[dy], partner)
@@ -276,89 +280,107 @@
         wd.append(cp)
     arrive_core(1, 2)
 
+    parts = ((away, 0, 64), (away, 64, 64), (home, 0, 128))
     aas, bs = {}, {}
     mycols = pl.ds(pl.multiple_of(zl * 128, 128), 128)
 
     def last_rows(zhalf):
-        row = pl.multiple_of(zhalf * 512, 512)
-        step(row, 512, video_pieces(1, 2), False)
-        rows = pl.ds(row, 512)
+        attend(zhalf, 1, 2)
+        rows = pl.ds(pl.multiple_of(zhalf * 512, 512), 512)
         att[rows, :] = (acc[rows, :] / jnp.sum(l_ref[rows, :], axis=1, keepdims=True)).astype(BF)
 
-    def send_att(zhalf, k):
-        for d in range(1, 4):
+    def send_att(k):
+        zhalf, r0, nr = parts[k]
+        for d in (2, 1, 3):
             zl1 = (zl + d) % 4
-            rows = pl.ds(pl.multiple_of(zhalf * 512 + zl1 * 128, 128), 128)
+            rows = pl.ds(pl.multiple_of(zhalf * 512 + zl1 * 128 + r0, 64), nr)
             cp = remote(
-                att.at[rows], abuf.at[zhalf, y, :, mycols], a_send.at[k, d], a_recv.at[k, d],
+                att.at[rows], abuf.at[zhalf, y, pl.ds(r0, nr), mycols], a_send.at[k, d], a_recv.at[k, d],
                 dev(x, y, zh, zl1, c),
             )
             cp.start()
             aas[(k, d)] = cp
-        rows = pl.ds(pl.multiple_of(zhalf * 512 + zl * 128, 128), 128)
-        abuf[zhalf, y, :, mycols] = att[rows, :]
-
-    def send_b(zhalf, k):
-        for d in range(1, 4):
-            aas[(k, d)].wait_recv()
-        piece = abuf.at[zhalf, y]
-        for dy in (2, 1, 3):
-            cp = remote(
-                piece, piece, b_send.at[k, dy], b_recv.at[k, dy], dev(x, (y + dy) % 4, zh, zl, c)
-            )
-            cp.start()
-            bs[(k, dy)] = cp
-
-    away, home = 1 - zh, zh
+        rows = pl.ds(pl.multiple_of(zhalf * 512 + zl * 128 + r0, 64), nr)
+        abuf[zhalf, y, r0 : r0 + nr, mycols] = att[rows, :]
+
+    def send_b(k):
+        zhalf, r0, nr = parts[k]
+        for d in (0, 1, 3, 2):
+            if d:
+                aas[(k, d)].wait_recv()
+            cols = pl.ds(pl.multiple_of(((zl + 4 - d) % 4) * 128, 128), 128)
+            piece = abuf.at[zhalf, y, pl.ds(r0, nr), cols]
+            for dy in (2, 1, 3):
+                cp = remote(
+                    piece, piece, b_send.at[k, d, dy], b_recv.at[k, d, dy],
+                    dev(x, (y + dy) % 4, zh, zl, c),
+                )
+                cp.start()
+                bs[(k, d, dy)] = cp
+
     last_rows(away)
-    send_att(away, 0)
+    send_att(0)
+    send_att(1)
+    attend(home, 1, 3)
+    send_b(0)
+    send_b(1)
     last_rows(home)
-    send_att(home, 1)
-    send_b(away, 0)
-    send_b(home, 1)
+    send_att(2)
+
+    send_b(2)
 
     for cp in wd:
         cp.wait_recv()
 
-    def part(zhalf, n):
+    def wait_b(k):
+        for d in range(4):
+            for dy in range(1, 4):
+                bs[(k, d, dy)].wait_recv()
+
+    def part(k, n):
+        zhalf, r0, nr = parts[k]
         tot = None
         for yy in range(4):
             t = jnp.dot(
-                abuf[zhalf, yy], wbuf[yy, :, n * CW : (n + 1) * CW], preferred_element_type=F32
+                abuf[zhalf, yy, r0 : r0 + nr], wbuf[yy, :, n * CW : (n + 1) * CW],
+                preferred_element_type=F32,
             )
             tot = t if tot is None else tot + t
         return tot
 
-    for dy in range(1, 4):
-        bs[(0, dy)].wait_recv()
-    zs = []
+    zs = {}
+    for k in (0, 1):
+        wait_b(k)
+        for n in range(NCH):
+            psend[k, n] = part(k, n).astype(BF)
+            zs[(k, n)] = remote(
+                psend.at[k, n], zbuf.at[k, n], z_send.at[k, n], z_recv.at[k, n],
+                dev(x, y, 1 - zh, zl, c),
+            )
+            zs[(k, n)].start()
+    wait_b(2)
     for n in range(NCH):
-        psend[n] = part(away, n).astype(BF)
-        cp = remote(psend.at[n], zbuf.at[n], z_send.at[n], z_recv.at[n], dev(x, y, 1 - zh, zl, c))
-        cp.start()
-        zs.append(cp)
-    for dy in range(1, 4):
-        bs[(1, dy)].wait_recv()
-    for n in range(NCH):
-        pown[n] = part(home, n)
-    os = []
-    for n in range(NCH):
-        zs[n].wait_recv()
-        osend[n] = (pown[n] + zbuf[n].astype(F32)).astype(BF)
-        for dy in (2, 1, 3):
-            y1 = (y + dy) % 4
-            cp = remote(
-                osend.at[n, pl.ds(pl.multiple_of(y1 * 32, 32), 32)],
-                out_ref.at[:, pl.ds(pl.multiple_of(y * COLS + n * CW, 128), CW)],
-                o_send.at[n, dy], o_recv.at[n, dy], dev(x, y1, zh, zl, c),
-            )
-            cp.start()
-            os.append(cp)
-        out_ref[:, pl.ds(pl.multiple_of(y * COLS + n * CW, 128), CW)] = osend[
-            n, pl.ds(pl.multiple_of(y * 32, 32), 32), :
-        ]
-
-    for cp in os:
+        pown[n] = part(2, n)
+    os = {}
+    for k in (0, 1):
+        for n in range(NCH):
+            cols = pl.ds(pl.multiple_of(y * COLS + n * CW, 128), CW)
+            zs[(k, n)].wait_recv()
+            osend[k, n] = (pown[n, k * 64 : (k + 1) * 64] + zbuf[k, n].astype(F32)).astype(BF)
+            for dy in (2, 1, 3):
+                y1 = (y + dy) % 4
+                cp = remote(
+                    osend.at[k, n, pl.ds(pl.multiple_of((y1 % 2) * 32, 32), 32)],
+                    out_ref.at[:, cols], o_send.at[n, dy], o_recv.at[n, dy], dev(x, y1, zh, zl, c),
+                )
+                pl.when(y1 // 2 == k)(cp.start)
+                os[(n, dy)] = cp
+
+            @pl.when(y // 2 == k)
+            def _(k=k, n=n, cols=cols):
+                out_ref[:, cols] = osend[k, n, pl.ds(pl.multiple_of((y % 2) * 32, 32), 32), :]
+
+    for cp in os.values():
         cp.wait_recv()
     for i in range(3):
         for half in range(2):
@@ -366,7 +388,8 @@
             total_wait(qbuf.at[pl.ds(0, n)], p1_send.at[i, half])
     for cp in (
         [t[0] for t in texts] + list(ws.values()) + wd + list(xs.values()) + list(ds.values())
-        + list(aas.values()) + list(bs.values()) + zs + os
+        + list(aas.values()) + list(bs.values())
+        + list(zs.values()) + list(os.values())
     ):
         cp.wait_send()
 
@@ -384,11 +407,11 @@
             vm((1024, 128), BF), vm((4, 2, 1024, 128), BF), vm((4, 2, 1024, 128), BF),
             vm((2, 2, 512, 128), BF), vm((4, 512, COLS), BF), vm((2, 4, 128, 512), BF),
             vm((1024, 128), BF), vm((1024, 128), F32), vm((1024, 128), F32), vm((1024, 128), F32),
-            vm((NCH, 128, CW), BF), vm((NCH, 128, CW), F32), vm((NCH, 128, CW), BF), vm((NCH, 128, CW), BF),
+            vm((2, NCH, 64, CW), BF), vm((NCH, 128, CW), F32), vm((2, NCH, 64, CW), BF), vm((2, NCH, 64, CW), BF),
             dma((9,)), dma((3, 2)), dma((3, 2)), dma((2, 2, 4)), dma((2, 2, 4)), dma((2, 2, 4)), dma((2, 2, 4)),
             dma((2,)), dma((2,)), dma((5,)), dma((5,)), dma((4,)), dma((4,)),
-            dma((2, 4)), dma((2, 4)), dma((2, 4)), dma((2, 4)),
-            dma((NCH,)), dma((NCH,)), dma((NCH, 4)), dma((NCH, 4)),
+            dma((3, 4)), dma((3, 4)), dma((3, 4, 4)), dma((3, 4, 4)),
+            dma((2, NCH)), dma((2, NCH)), dma((NCH, 4)), dma((NCH, 4)),
         ],
         compiler_params=pltpu.CompilerParams(
             collective_id=0, has_side_effects=True, vmem_limit_bytes=60 * 1024 * 1024

time: 79.7 us -> 78.4 us (0.984)
  the two profiles are of different devices: /device:TPU:2 before, /device:TPU:88 now
where the time goes in v4:
time: 78.4 us; the launch traced here: 78.3 us
  Pallas kernels  76.6 us (98%)
  local copies, waits for them, and re-layouts  1.72 us (2%)
    pallas_call x1, Pallas kernels, body(): pl.pallas_call(kernel, out_shape=jax.ShapeDtypeStruct((32, 5120), BF), in...  76.6 us
    unnamed x1, local copies, waits for them, and re-layouts  1.72 us

profile of v4, /device:TPU:88, one launch (start us, length us, event | category | flops | bytes accessed | tf_op | source)
XLA Modules:
  0.0 78.3 jit_solution(9559893202202821900)
XLA Ops:
  0.0 76.6 %shard_map.64 = bf16[32,5120]{1,0:T(8,128)(2,1)} custom-call(bf16[32,4096]{1,0:T(8,128)(2,1)} %q_hbm.1, bf16[32,4096]{1,0:T(8,128)(2,1)} %k_hbm.1, bf16[32,4096]{1,0:T(8,128)(2,1)} %v_hbm.1, bf16[512,256]{1,0:T(8,128)(2,1)} %tk_hbm.1, bf16[512,256]{1,0:T(8,128)(2,1)} %tv_hbm.1, bf16[256,5120]{1,0:T(8,128)(2,1)} %w_hbm.1), custom_call_target="tpu_custom_call" | custom-call | tf_op jit(solution)/shard_map/pallas_call | solution.py:400
  76.6 1.7 %copy.8 = bf16[32,5120]{1,0:T(8,128)(2,1)} copy(bf16[32,5120]{1,0:T(8,128)(2,1)} %shard_map.64) | data formatting | bytes 655360
